TPU v7x, 32 devices: a whole 2x2x4 slice. The times are simulated.
32 devices in a mesh: aa: 4 (over x, core), ba: 8 (over z, y).
Axes of the slice: x: 2, y: 2, z: 4, core: 2. Of those that a mesh axis runs over, the one named last changes fastest.
Arguments:
- activations: bfloat16 [1024, 4224], P('aa', 'ba'), may hold values from -6 to 6
- out_grad: bfloat16 [1024, 4096], P('aa', 'ba'), may hold values from -0.1875 to 0.1875
- momentum: float32 [4224, 4096], P('aa', 'ba'), may hold values from -6 to 6
- weight: float32 [4224, 4096], P('aa', 'ba'), may hold values from -6 to 6
- norm_scale: float32 [], replicated, may hold values from 128.99231 to 257.98462
- step_size: float32 [], replicated, may hold values from 0.5 to 2
Outputs:
- new_weight: float32 [4224, 4096], P('aa', 'ba')
- new_momentum: float32 [4224, 4096], P('aa', 'ba')
All inputs are finite; a program needn't handle non-finite values.
Results may differ from a plain program's by a relative error of at most 0.00068.
Values may be sent and summed in bfloat16 or wider, within the bound.
A program may use at most 64 MiB of HBM per device.

v0:
```python
import math

import jax
import jax.numpy as jnp
from jax import lax
from jax.sharding import PartitionSpec as P

ROWS = 4224
COLS = 4096


def inner_rows(left, right):
    return lax.dot_general(
        left, right, (((0,), (0,)), ((), ())), preferred_element_type=jnp.float32
    )


def per_device(activations, out_grad, momentum, weight, norm_scale, step_size):
    partial_term = inner_rows(lax.all_gather(activations, "ba", axis=1, tiled=True), out_grad)
    gradient = lax.psum_scatter(partial_term, "aa", scatter_dimension=0, tiled=True)
    new_momentum = 0.95 * momentum + gradient
    scaled = (new_momentum / norm_scale).astype(jnp.bfloat16)
    row_panel = lax.all_gather(scaled, "ba", axis=1, tiled=True)
    gram_part = inner_rows(row_panel, scaled)
    width = gram_part.shape[0]
    groups = lax.axis_size("aa")
    padding = (groups - width % groups) % groups
    padded = jnp.pad(gram_part, ((0, padding), (0, 0)))
    share = lax.psum_scatter(padded, "aa", scatter_dimension=0, tiled=True).astype(jnp.bfloat16)
    gram_cols = lax.all_gather(share, "aa", axis=0, tiled=True)[:width]
    first_power = jnp.dot(row_panel, gram_cols, preferred_element_type=jnp.float32).astype(
        jnp.bfloat16
    )
    second_power = jnp.dot(
        lax.all_gather(first_power, "ba", axis=1, tiled=True),
        gram_cols,
        preferred_element_type=jnp.float32,
    )
    direction = (
        3.4445 * scaled.astype(jnp.float32)
        - 4.775 * first_power.astype(jnp.float32)
        + 2.0315 * second_power
    )
    factor = 0.2 * math.sqrt(max(ROWS, COLS))
    new_weight = weight - step_size * factor * direction
    return (new_weight, new_momentum)


def solution(mesh):
    placed = (P("aa", "ba"), P("aa", "ba"), P("aa", "ba"), P("aa", "ba"), P(), P())
    return jax.shard_map(
        per_device,
        mesh=mesh,
        in_specs=placed,
        out_specs=(P("aa", "ba"), P("aa", "ba")),
        check_vma=False,
    )
```

profile of v0, /device:TPU:0, one launch (start us, length us, event | category | flops | bytes accessed | tf_op | source)
XLA Modules:
  0.0 547.1 jit_solution(9416157465586659911)
XLA Ops:
  7.2 0.0 copy-start
  7.2 0.0 all-gather.5.cloned.1.call-start
  7.2 0.7 all-gather.5.cloned.1.call-update
  7.9 0.0 reduce-scatter.3.cloned.1.call-start
  8.0 54.8 %all-gather.5.cloned.1.call-done = bf16[256,4224]{0,1:T(8,128)(2,1)} async-done(((bf16[256,528]{0,1:T(8,128)(2,1)}), bf16[256,4224]{0,1:T(8,128)(2,1)}) %all-gather.5.cloned.1.call-update) | async-done | bytes 2162704 | tf_op jit(solution)/shard_map/all_gather | solution.py:19
  62.7 0.0 copy-done
  62.7 6.2 %fusion.3 = f32[4224,512]{1,0:T(8,128)} fusion(bf16[256,4224]{0,1:T(8,128)(2,1)} %all-gather.5.cloned.1.call-done, bf16[256,512]{1,0:T(8,128)(2,1)S(1)} %copy-done), kind=kOutput, calls=%fused_computation.7 | convolution fusion | flops 1107296256 | bytes 11075584 | tf_op jit(solution)/shard_map/dot_general | solution.py:13
  69.0 0.0 copy-start.2
  69.0 0.0 reduce-scatter.3.cloned.1.call-update
  69.0 0.0 all-gather.7.cloned.1.call-start
  69.8 70.9 %reduce-scatter.3.cloned.1.call-done = f32[1056,512]{1,0:T(8,128)} async-done(((f32[4224,512]{1,0:T(8,128)}), f32[1056,512]{1,0:T(8,128)}) %reduce-scatter.3.cloned.1.call-update) | async-done | bytes 2162704 | tf_op jit(solution)/shard_map/reduce_scatter | solution.py:20
  140.7 0.0 copy-done.2
  140.7 3.9 divide_convert_fusion
  144.6 0.0 all-gather.7.cloned.1.call-update
  144.6 0.0 reduce-scatter.5.cloned.1.call-start
  144.6 128.2 %all-gather.7.cloned.1.call-done = bf16[1056,4096]{1,0:T(8,128)(2,1)} async-done(((bf16[1056,512]{1,0:T(8,128)(2,1)}), bf16[1056,4096]{1,0:T(8,128)(2,1)}) %all-gather.7.cloned.1.call-update) | async-done | bytes 8650768 | tf_op jit(solution)/shard_map/all_gather | solution.py:23
  272.9 10.3 %fusion.4 = f32[4096,512]{1,0:T(8,128)} fusion(bf16[1056,4096]{1,0:T(8,128)(2,1)} %all-gather.7.cloned.1.call-done, bf16[1056,512]{1,0:T(8,128)(2,1)} %get-tuple-element.2), kind=kOutput, calls=%fused_computation.8 | convolution fusion | flops 4429185024 | bytes 18120704 | tf_op jit(solution)/shard_map/dot_general | solution.py:13
  283.2 0.0 reduce-scatter.5.cloned.1.call-update
  283.2 0.0 all-gather.9.cloned.1.call-start
  283.3 69.7 %reduce-scatter.5.cloned.1.call-done = f32[1024,512]{1,0:T(8,128)} async-done(((f32[4096,512]{1,0:T(8,128)}), f32[1024,512]{1,0:T(8,128)}) %reduce-scatter.5.cloned.1.call-update) | async-done | bytes 2097168 | tf_op jit(solution)/shard_map/reduce_scatter | solution.py:29
  353.0 2.7 convert_element_type.17
  355.7 0.0 all-gather.9.cloned.1.call-update
  355.7 0.0 copy-start.1
  355.7 0.0 copy-start.3
  355.7 0.0 all-gather.11.cloned.1.call-start
  355.8 34.5 %all-gather.9.cloned.1.call-done = bf16[4096,512]{1,0:T(8,128)(2,1)} async-done(((bf16[1024,512]{1,0:T(8,128)(2,1)}), bf16[4096,512]{1,0:T(8,128)(2,1)}) %all-gather.9.cloned.1.call-update) | async-done | bytes 4194320 | tf_op jit(solution)/shard_map/all_gather | solution.py:30
  390.3 10.3 %convolution_convert_fusion = bf16[1056,512]{1,0:T(8,128)(2,1)} fusion(bf16[1056,4096]{1,0:T(8,128)(2,1)} %all-gather.7.cloned.1.call-done, bf16[4096,512]{1,0:T(8,128)(2,1)} %all-gather.9.cloned.1.call-done), kind=kOutput, calls=%fused_computation.4 | convolution fusion | flops 4429725696 | bytes 13926400 | tf_op jit(solution)/shard_map/dot_general | solution.py:31
  400.6 0.0 all-gather.11.cloned.1.call-update
  401.3 127.6 %all-gather.11.cloned.1.call-done = bf16[1056,4096]{1,0:T(8,128)(2,1)} async-done(((bf16[1056,512]{1,0:T(8,128)(2,1)}), bf16[1056,4096]{1,0:T(8,128)(2,1)}) %all-gather.11.cloned.1.call-update) | async-done | bytes 8650768 | tf_op jit(solution)/shard_map/all_gather | solution.py:35
  529.0 0.0 copy-done.1
  529.0 0.0 copy-done.3
  529.0 11.3 %fusion.2 = f32[1056,512]{1,0:T(8,128)} fusion(f32[1056,512]{1,0:T(8,128)S(1)} %copy-done.3, bf16[1056,4096]{1,0:T(8,128)(2,1)} %all-gather.11.cloned.1.call-done, bf16[4096,512]{1,0:T(8,128)(2,1)} %all-gather.9.cloned.1.call-done, bf16[1056,512]{1,0:T(8,128)(2,1)} %convolution_convert_fusion, bf16[1056,512]{1,0:T(8,128)(2,1)S(1)} %copy-done.1, f32[]{:T(128)S(6)} %mul.33), kind=kOutput, calls=%fused_computation.3 | convolution fusion | flops 4434051072 | bytes 19333124 | tf_op jit(solution)/shard_map/dot_general | solution.py:34
Async XLA Ops:
  7.2 55.6 %copy-start = (bf16[256,512]{1,0:T(8,128)(2,1)S(1)}, bf16[256,512]{1,0:T(8,128)(2,1)}, u32[]{:S(2)}) copy-start(bf16[256,512]{1,0:T(8,128)(2,1)} %param.7) | copy-start | bytes 786436
  7.2 55.5 %all-gather.5.cloned.1.call-start = ((), (), s32[]{:S(2)}) async-start(), calls=%async_computation.2 | async-start | bytes 2433024 | tf_op jit(solution)/shard_map/all_gather | solution.py:19
  7.9 132.8 %reduce-scatter.3.cloned.1.call-start = ((), (), s32[]{:S(2)}) async-start(), calls=%async_computation.3 | async-start | bytes 10813440 | tf_op jit(solution)/shard_map/reduce_scatter | solution.py:20
  69.0 71.7 %copy-start.2 = (f32[1056,512]{1,0:T(8,128)S(1)}, f32[1056,512]{1,0:T(8,128)}, u32[]{:S(2)}) copy-start(f32[1056,512]{1,0:T(8,128)} %param.8) | copy-start | bytes 6488068
  69.0 203.9 %all-gather.7.cloned.1.call-start = ((), (), s32[]{:S(2)}) async-start(), calls=%async_computation.4 | async-start | bytes 9732096 | tf_op jit(solution)/shard_map/all_gather | solution.py:23
  144.6 208.4 %reduce-scatter.5.cloned.1.call-start = ((), (), s32[]{:S(2)}) async-start(), calls=%async_computation.5 | async-start | bytes 10485760 | tf_op jit(solution)/shard_map/reduce_scatter | solution.py:29
  283.2 107.1 %all-gather.9.cloned.1.call-start = ((), (), s32[]{:S(2)}) async-start(), calls=%async_computation.6 | async-start | bytes 5242880 | tf_op jit(solution)/shard_map/all_gather | solution.py:30
  355.7 173.2 %copy-start.1 = (bf16[1056,512]{1,0:T(8,128)(2,1)S(1)}, bf16[1056,512]{1,0:T(8,128)(2,1)}, u32[]{:S(2)}) copy-start(bf16[1056,512]{1,0:T(8,128)(2,1)} %get-tuple-element.2) | copy-start | bytes 3244036
  355.7 173.2 %copy-start.3 = (f32[1056,512]{1,0:T(8,128)S(1)}, f32[1056,512]{1,0:T(8,128)}, u32[]{:S(2)}) copy-start(f32[1056,512]{1,0:T(8,128)} %param.9) | copy-start | bytes 6488068
  355.7 173.2 %all-gather.11.cloned.1.call-start = ((), (), s32[]{:S(2)}) async-start(), calls=%async_computation.7 | async-start | bytes 9732096 | tf_op jit(solution)/shard_map/all_gather | solution.py:35
Sparse Core Ops, SparseCore 0:
  10.2 52.5 all-gather.4
  69.1 71.5 reduce-scatter.2
  144.7 128.1 all-gather.6
  283.4 69.5 reduce-scatter.4
  355.8 34.4 all-gather.8
  400.8 128.1 all-gather.10
where the time goes:
time: 547 us
  waiting for transfers between devices  486 us (89%)
  matrix products  38.2 us (7%)
  between operations  15.6 us (3%)
  other arithmetic  6.59 us (1%)
    all_gather x1, waiting for transfers between devices, per_device(): row_panel = lax.all_gather(scaled, 'ba', axis=1, tiled=True)  128 us
    all_gather x1, waiting for transfers between devices, per_device(): lax.all_gather(first_power, 'ba', axis=1, tiled=True)  128 us
    reduce_scatter x1, waiting for transfers between devices, per_device(): lax.psum_scatter(partial_term, 'aa', scatter_dimension=0, tiled=True)  70.9 us
    reduce_scatter x1, waiting for transfers between devices, per_device(): lax.psum_scatter(padded, 'aa', scatter_dimension=0, tiled=True)  69.7 us
    all_gather x1, waiting for transfers between devices, per_device(): lax.all_gather(activations, 'ba', axis=1, tiled=True)  54.8 us
    all_gather x1, waiting for transfers between devices, per_device(): gram_cols = lax.all_gather(share, 'aa', axis=0, tiled=True)[:width]  34.5 us
    dot_general x2, matrix products, inner_rows(): lax.dot_general(left, right, (((0,), (0,)), ((), ())), preferred_element_...  16.6 us
    dot_general x1, matrix products, per_device(): jnp.dot(lax.all_gather(first_power, 'ba', axis=1, tiled=True), gram_cols,...  11.3 us
  transfers between devices with their start and end apart: 6, of which 6 were waited for; matrix products, arithmetic and copies ran while one was open for 0% of the time, Pallas kernels for 0%

commit v1 on v0

--- a/solution.py
+++ b/solution.py
@@ -1,12 +1,16 @@
+import functools
 import math
 
 import jax
 import jax.numpy as jnp
 from jax import lax
+from jax.experimental import pallas as pl
+from jax.experimental.pallas import tpu as pltpu
 from jax.sharding import PartitionSpec as P
 
 ROWS = 4224
 COLS = 4096
+MESH = pl.DeviceIdType.MESH
 
 
 def inner_rows(left, right):
@@ -15,11 +19,218 @@
     )
 
 
-def per_device(activations, out_grad, momentum, weight, norm_scale, step_size):
-    partial_term = inner_rows(lax.all_gather(activations, "ba", axis=1, tiled=True), out_grad)
-    gradient = lax.psum_scatter(partial_term, "aa", scatter_dimension=0, tiled=True)
-    new_momentum = 0.95 * momentum + gradient
-    scaled = (new_momentum / norm_scale).astype(jnp.bfloat16)
+def powers_kernel(
+    n, groups, x_ref, out_ref,
+    panel, powers, own_power, gram, parts, from_core, from_chip,
+    x_send, x_recv, y_send, y_recv, c_send, c_recv, p_send, p_recv, s_send, s_recv,
+):
+    rows, width = x_ref.shape
+    half, share, middle = rows // 2, width // groups, n // 2
+    a, b = lax.axis_index("aa"), lax.axis_index("ba")
+    core_mate = a + 1 - 2 * (a % 2)
+    chip_mate = (a + 2) % groups
+
+    place = b // 2 + (b % 2) * (n - 1 - 2 * (b // 2))
+
+    def at(position):
+        position = (position + n) % n
+        column = position // middle
+        return 2 * (position + column * (n - 1 - 2 * position)) + column
+
+    neighbours = (at(place + 1), at(place - 1))
+
+    barrier = pltpu.get_barrier_semaphore()
+    for d in range(2):
+        pl.semaphore_signal(barrier, 1, device_id={"ba": neighbours[d]}, device_id_type=MESH)
+    for mate in (core_mate, chip_mate):
+        pl.semaphore_signal(barrier, 1, device_id={"aa": mate}, device_id_type=MESH)
+    pl.semaphore_wait(barrier, 4)
+
+    def hop(own, held, send, recv, d, s, k):
+        target = n - 1 if s == middle else 2 * s - 1 + d
+        part = pl.ds(k * half, half)
+        source = own.at[part] if s == 1 else held.at[2 * s - 3 + d, part]
+        return pltpu.make_async_remote_copy(
+            src_ref=source, dst_ref=held.at[target, part],
+            send_sem=send.at[d, s - 1, k], recv_sem=recv.at[d, s - 1, k],
+            device_id={"ba": neighbours[d]}, device_id_type=MESH,
+        )
+
+    def hops(s):
+        return [(k, d) for k in range(2) for d in range(2) if s < middle or k == d]
+
+    def ring(own, held, send, recv, use):
+        for s in range(1, middle + 1):
+            for k, d in hops(s):
+                hop(own, held, send, recv, d, s, k).wait_recv()
+                if s < middle and (k, d) in hops(s + 1):
+                    hop(own, held, send, recv, d, s + 1, k).start()
+            use([2 * s - 1, 2 * s] if s < middle else [n - 1])
+
+    def drain(own, held, send, recv):
+        for s in range(1, middle + 1):
+            for k, d in hops(s):
+                hop(own, held, send, recv, d, s, k).wait_send()
+
+    def share_rows(index):
+        return pl.ds(pl.multiple_of(index * share, share), share)
+
+    def to_mate(source, target, send, recv, mate):
+        return pltpu.make_async_remote_copy(
+            src_ref=source, dst_ref=target, send_sem=send, recv_sem=recv,
+            device_id={"aa": mate}, device_id_type=MESH,
+        )
+
+    def core_copy(e):
+        return to_mate(
+            parts.at[e, pl.ds(2, 2)], from_core.at[e], c_send.at[e], c_recv.at[e], core_mate
+        )
+
+    def chip_copy(e):
+        return to_mate(parts.at[e, 1], from_chip.at[e], p_send.at[e], p_recv.at[e], chip_mate)
+
+    def share_copy(e, step):
+        mine = gram.at[e, share_rows(chip_mate if step == 2 else a)]
+        return to_mate(
+            mine, mine, s_send.at[e, step], s_recv.at[e, step],
+            chip_mate if step == 0 else core_mate,
+        )
+
+    def block(e):
+        return x_ref if e == 0 else panel.at[e]
+
+    def gram_partial(e):
+        @pl.loop(0, 4)
+        def _(r):
+            owner = (a + (r // 2) * (1 - 2 * (a % 2)) + 2 * (r % 2)) % groups
+            parts[e, r] = inner_rows(block(e)[:, share_rows(owner)], x_ref[...])
+
+        core_copy(e).start()
+
+    def core_sum(e):
+        core_copy(e).wait_recv()
+        parts[e, 1] = parts[e, 1] + from_core[e, 1]
+        chip_copy(e).start()
+        parts[e, 0] = parts[e, 0] + from_core[e, 0]
+
+    def gram_share(e):
+        chip_copy(e).wait_recv()
+        gram[e, share_rows(a)] = (parts[e, 0] + from_chip[e]).astype(jnp.bfloat16)
+        share_copy(e, 0).start()
+        share_copy(e, 1).start()
+
+    def relay(e):
+        share_copy(e, 0).wait_recv()
+        share_copy(e, 2).start()
+
+    def gram_ready(e):
+        share_copy(e, 1).wait_recv()
+        share_copy(e, 2).wait_recv()
+
+    def accumulate(e, source, first, start, count):
+        tile = count // 3 if count % 48 == 0 else count
+
+        @pl.loop(0, count // tile)
+        def _(t):
+            part = pl.ds(pl.multiple_of(start + t * tile, 16), tile)
+            term = jnp.dot(source[part, :], gram[e], preferred_element_type=jnp.float32)
+            if first:
+                out_ref[part, :] = term
+            else:
+                out_ref[part, :] += term
+
+    for k, d in hops(1):
+        hop(x_ref, panel, x_send, x_recv, d, 1, k).start()
+    gram_partial(0)
+    core_sum(0)
+    summed, shared = [0], []
+
+    def use_block(events):
+        for e in events:
+            gram_partial(e)
+        for e in events:
+            core_sum(e)
+        for e in summed:
+            gram_share(e)
+        for e in shared:
+            relay(e)
+        shared[:] = summed
+        summed[:] = events
+
+    ring(x_ref, panel, x_send, x_recv, use_block)
+
+    for e in range(n):
+        if e == n - 4:
+            gram_share(n - 1)
+        if e in shared:
+            relay(e)
+        if e == n - 1:
+            relay(e)
+        gram_ready(e)
+        if e < n - 1:
+            accumulate(e, block(e), e == 0, 0, rows)
+    for k in range(2):
+        accumulate(n - 1, block(n - 1), False, k * half, half)
+        part = pl.ds(k * half, half)
+        own_power[part, :] = out_ref[part, :].astype(jnp.bfloat16)
+        for d in range(2):
+            hop(own_power, powers, y_send, y_recv, d, 1, k).start()
+
+    def power_block(e):
+        return own_power if e == 0 else powers.at[e]
+
+    accumulate(0, own_power, True, 0, rows)
+
+    def use_power(events):
+        for e in events:
+            accumulate(e, power_block(e), False, 0, rows)
+
+    ring(own_power, powers, y_send, y_recv, use_power)
+    out_ref[...] = (
+        3.4445 * x_ref[...].astype(jnp.float32)
+        - 4.775 * own_power[...].astype(jnp.float32)
+        + 2.0315 * out_ref[...]
+    )
+    drain(x_ref, panel, x_send, x_recv)
+    drain(own_power, powers, y_send, y_recv)
+    for e in range(n):
+        core_copy(e).wait_send()
+        chip_copy(e).wait_send()
+        for step in range(3):
+            share_copy(e, step).wait_send()
+
+
+def fused_direction(scaled, n, groups):
+    rows, width = scaled.shape
+    share = width // groups
+    middle = n // 2
+    dma = pltpu.SemaphoreType.DMA
+    return pl.pallas_call(
+        functools.partial(powers_kernel, n, groups),
+        out_shape=jax.ShapeDtypeStruct((rows, width), jnp.float32),
+        in_specs=[pl.BlockSpec(memory_space=pltpu.VMEM)],
+        out_specs=pl.BlockSpec(memory_space=pltpu.VMEM),
+        scratch_shapes=[
+            pltpu.VMEM((n, rows, width), jnp.bfloat16),
+            pltpu.VMEM((n, rows, width), jnp.bfloat16),
+            pltpu.VMEM((rows, width), jnp.bfloat16),
+            pltpu.VMEM((n, width, width), jnp.bfloat16),
+            pltpu.VMEM((n, 4, share, width), jnp.float32),
+            pltpu.VMEM((n, 2, share, width), jnp.float32),
+            pltpu.VMEM((n, share, width), jnp.float32),
+            dma((2, middle, 2)), dma((2, middle, 2)),
+            dma((2, middle, 2)), dma((2, middle, 2)),
+            dma((n,)), dma((n,)), dma((n,)), dma((n,)),
+            dma((n, 3)), dma((n, 3)),
+        ],
+        compiler_params=pltpu.CompilerParams(
+            collective_id=0, has_side_effects=True, vmem_limit_bytes=62 * 1024 * 1024
+        ),
+        name="powers",
+    )(scaled)
+
+
+def plain_direction(scaled):
     row_panel = lax.all_gather(scaled, "ba", axis=1, tiled=True)
     gram_part = inner_rows(row_panel, scaled)
     width = gram_part.shape[0]
@@ -36,11 +247,30 @@
         gram_cols,
         preferred_element_type=jnp.float32,
     )
-    direction = (
+    return (
         3.4445 * scaled.astype(jnp.float32)
         - 4.775 * first_power.astype(jnp.float32)
         + 2.0315 * second_power
     )
+
+
+def per_device(activations, out_grad, momentum, weight, norm_scale, step_size):
+    features = lax.all_to_all(
+        lax.all_gather(activations, "ba", axis=1, tiled=True),
+        "aa", split_axis=1, concat_axis=0, tiled=True,
+    )
+    gradient = inner_rows(features, lax.all_gather(out_grad, "aa", axis=0, tiled=True))
+    new_momentum = 0.95 * momentum + gradient
+    scaled = (new_momentum / norm_scale).astype(jnp.bfloat16)
+    n, groups = lax.axis_size("ba"), lax.axis_size("aa")
+    rows, width = scaled.shape
+    fits = (
+        n % 2 == 0 and n >= 4 and width % 128 == 0
+        and width % (16 * groups) == 0 and rows % 32 == 0 and groups == 4
+        and (width // groups) % 128 == 0
+        and 4 * n * rows * width + 9 * n * width * width + 9 * rows * width < 56 * 2**20
+    )
+    direction = fused_direction(scaled, n, groups) if fits else plain_direction(scaled)
     factor = 0.2 * math.sqrt(max(ROWS, COLS))
     new_weight = weight - step_size * factor * direction
     return (new_weight, new_momentum)

time: 547 us -> 320 us (0.59)
  waiting for transfers between devices: 486 us -> 86.1 us
  Pallas kernels: 0 us -> 202 us
  matrix products: 38.2 us -> 5.58 us
    all_gather x3 -> x1, waiting for transfers between devices: 290 us -> 0.01 us  [per_device(): lax.all_gather(out_grad, 'aa', axis=0, tiled=True)]
    pallas_call x0 -> x1, Pallas kernels: none -> 202 us  [fused_direction(): pl.pallas_call(functools.partial(powers_kernel, n, groups), out_shape=jax...]
    reduce_scatter x2 -> x0, waiting for transfers between devices: 141 us -> none  [the longest x1 70.9 us: per_device(): lax.psum_scatter(partial_term, 'aa', scatter_dimension=0, tiled=True)]
    all_to_all x0 -> x1, waiting for transfers between devices: none -> 30.1 us  [per_device(): lax.all_to_all(lax.all_gather(activations, 'ba', axis=1, tiled=True), 'aa...]
    dot_general x2 -> x0, matrix products: 21.6 us -> none  [the longest x1 11.3 us: per_device(): jnp.dot(lax.all_gather(first_power, 'ba', axis=1, tiled=True), gram_cols,...]
    dot_general x2 -> x1, matrix products: 16.6 us -> 5.58 us  [inner_rows(): lax.dot_general(left, right, (((0,), (0,)), ((), ())), preferred_element_...]
    convert_element_type x2 -> x0, other arithmetic: 6.59 us -> none  [the longest x1 3.87 us: per_device(): scaled = (new_momentum / norm_scale).astype(jnp.bfloat16)]
  transfers between devices with their start and end apart: 6 -> 3, of which waited for: 6 -> 2; matrix products, arithmetic and copies ran while one was open for 0% -> 1% of each run, Pallas kernels for 0% -> 0%
where the time goes in v1:
time: 320 us
  Pallas kernels  202 us (63%)
  waiting for transfers between devices  86.1 us (27%)
  between operations  16.8 us (5%)
  matrix products  5.58 us (2%)
  other arithmetic  4.11 us (1%)
  starting transfers between devices  3.69 us (1%)
    pallas_call x1, Pallas kernels, fused_direction(): pl.pallas_call(functools.partial(powers_kernel, n, groups), out_shape=jax...  202 us
    all_gather x1, waiting for transfers between devices, per_device(): lax.all_gather(activations, 'ba', axis=1, tiled=True)  54.8 us
    all_to_all x1, waiting for transfers between devices, per_device(): lax.all_to_all(lax.all_gather(activations, 'ba', axis=1, tiled=True), 'aa...  30.1 us
  transfers between devices with their start and end apart: 3, of which 2 were waited for; matrix products, arithmetic and copies ran while one was open for 1% of the time, Pallas kernels for 0%

profile of v1, /device:TPU:0, one launch (start us, length us, event | category | flops | bytes accessed | tf_op | source)
XLA Modules:
  0.0 320.2 jit_solution(9665551982115453869)
XLA Ops:
  8.0 0.0 all-gather.3.cloned.1.call-start
  8.0 0.7 all-gather.3.cloned.1.call-update
  8.7 54.8 %all-gather.3.cloned.1.call-done = bf16[256,4224]{0,1:T(8,128)(2,1)} async-done(((bf16[256,528]{0,1:T(8,128)(2,1)}), bf16[256,4224]{0,1:T(8,128)(2,1)}) %all-gather.3.cloned.1.call-update) | async-done | bytes 2162704 | tf_op jit(solution)/shard_map/all_gather | solution.py:259
  63.5 3.6 %all-to-all-start = ((bf16[256,4,1056]{0,2,1:T(8,128)(2,1)}), bf16[256,4,1056]{0,2,1:T(8,128)(2,1)S(1)}, u32[]{:S(2)}, u32[]{:S(2)}) async-start(bf16[256,4,1056]{0,2,1:T(8,128)(2,1)} %bitcast.7), calls=%async_computation | async-start | bytes 4325376 | tf_op jit(solution)/shard_map/all_to_all | solution.py:258
  67.2 0.0 all-gather.5.cloned.1.call-start
  67.2 0.5 all-gather.5.cloned.1.call-update
  69.0 30.1 %all-to-all-done = bf16[256,4,1056]{0,2,1:T(8,128)(2,1)S(1)} async-done(((bf16[256,4,1056]{0,2,1:T(8,128)(2,1)}), bf16[256,4,1056]{0,2,1:T(8,128)(2,1)S(1)}, u32[]{:S(2)}, u32[]{:S(2)}) %all-to-all-start) | async-done | bytes 2162720 | tf_op jit(solution)/shard_map/all_to_all | solution.py:258
  99.1 1.6 copy.10
  100.8 0.0 all-gather.5.cloned.1.call-done
  100.8 5.6 %divide_convert_fusion = (bf16[1056,512]{1,0:T(8,128)(2,1)}, f32[1056,512]{1,0:T(8,128)}) fusion(f32[]{:T(128)S(6)} %copy.11, bf16[1024,1056]{0,1:T(8,128)(2,1)} %bitcast.8, bf16[1024,512]{1,0:T(8,128)(2,1)} %all-gather.5.cloned.1.call-done, f32[1056,512]{1,0:T(8,128)} %param.8), kind=kOutput, calls=%fused_computation.2 | convolution fusion | flops 1109458944 | bytes 8617988 | tf_op jit(solution)/shard_map/dot_general | solution.py:17
  106.3 202.3 %powers.1 = f32[1056,512]{1,0:T(8,128)} custom-call(bf16[1056,512]{1,0:T(8,128)(2,1)} %get-tuple-element.2.x_ref), custom_call_target="tpu_custom_call" | custom-call | tf_op jit(solution)/shard_map/powers/pallas_call | solution.py:208
  308.7 4.1 %multiply_subtract_fusion = f32[1056,512]{1,0:T(8,128)} fusion(f32[1056,512]{1,0:T(8,128)} %param.9, f32[1056,512]{1,0:T(8,128)} %powers.1, f32[]{:T(128)S(6)} %mul.15), kind=kLoop, calls=%fused_computation.1 | loop fusion | flops 1081344 | bytes 6488068 | tf_op jit(solution)/shard_map/sub | solution.py:275
Async XLA Ops:
  8.0 55.5 %all-gather.3.cloned.1.call-start = ((), (), s32[]{:S(2)}) async-start(), calls=%async_computation.1 | async-start | bytes 2433024 | tf_op jit(solution)/shard_map/all_gather | solution.py:259
  63.5 35.6 %all-to-all-start = ((bf16[256,4,1056]{0,2,1:T(8,128)(2,1)}), bf16[256,4,1056]{0,2,1:T(8,128)(2,1)S(1)}, u32[]{:S(2)}, u32[]{:S(2)}) async-start(bf16[256,4,1056]{0,2,1:T(8,128)(2,1)} %bitcast.7), calls=%async_computation | async-start | bytes 4325376 | tf_op jit(solution)/shard_map/all_to_all | solution.py:258
  67.2 33.6 %all-gather.5.cloned.1.call-start = ((), (), s32[]{:S(2)}) async-start(), calls=%async_computation.2 | async-start | bytes 1310720 | tf_op jit(solution)/shard_map/all_gather | solution.py:262
Sparse Core Ops, SparseCore 0:
  11.0 52.5 all-gather.2
Sparse Core Ops, SparseCore 1:
  69.2 21.3 all-gather.4

commit v2 on v1

--- a/solution.py
+++ b/solution.py
@@ -230,6 +230,152 @@
     )(scaled)
 
 
+def tokens_kernel(
+    n, groups, act_ref, grad_ref, act_out, grad_out,
+    held, tiles, grads, h_send, h_recv, t_send, t_recv, g_send, g_recv,
+):
+    middle, half = n // 2, act_ref.shape[0] // 2
+    a, b = lax.axis_index("aa"), lax.axis_index("ba")
+    place = b // 2 + (b % 2) * (n - 1 - 2 * (b // 2))
+
+    def at(position):
+        position = (position + n) % n
+        column = position // middle
+        return 2 * (position + column * (n - 1 - 2 * position)) + column
+
+    neighbours = (at(place + 1), at(place - 1))
+    peers = [(a + r) % groups for r in range(groups)]
+    barrier = pltpu.get_barrier_semaphore()
+    for d in range(2):
+        pl.semaphore_signal(barrier, 1, device_id={"ba": neighbours[d]}, device_id_type=MESH)
+    for r in range(1, groups):
+        pl.semaphore_signal(barrier, 1, device_id={"aa": peers[r]}, device_id_type=MESH)
+    pl.semaphore_wait(barrier, groups + 1)
+
+    def hop(d, s, k):
+        target = n - 1 if s == middle else 2 * s - 1 + d
+        part = pl.ds(k * half, half)
+        source = act_ref.at[part] if s == 1 else held.at[2 * s - 3 + d, part]
+        return pltpu.make_async_remote_copy(
+            src_ref=source, dst_ref=held.at[target, part],
+            send_sem=h_send.at[d, s - 1, k], recv_sem=h_recv.at[d, s - 1, k],
+            device_id={"ba": neighbours[d]}, device_id_type=MESH,
+        )
+
+    def hops(s):
+        return [(k, d) for k in range(2) for d in range(2) if s < middle or k == d]
+
+    def grad_copy(r):
+        return pltpu.make_async_remote_copy(
+            src_ref=grad_ref, dst_ref=grads.at[a],
+            send_sem=g_send.at[r], recv_sem=g_recv.at[r],
+            device_id={"aa": peers[r]}, device_id_type=MESH,
+        )
+
+    def block(e):
+        return act_ref if e == 0 else held.at[e]
+
+    def owner(e):
+        if e == 0:
+            return b
+        if e == n - 1:
+            return at(place + middle)
+        s = (e + 1) // 2
+        return at(place - s) if e % 2 else at(place + s)
+
+    def tile_copy(e):
+        index = owner(e)
+        return pltpu.make_async_remote_copy(
+            src_ref=block(e), dst_ref=tiles.at[index % 2, a],
+            send_sem=t_send.at[e], recv_sem=t_recv.at[index % 2, a],
+            device_id={"aa": index // 2}, device_id_type=MESH,
+        )
+
+    def deliver(e):
+        index = owner(e)
+
+        @pl.when(index // 2 != a)
+        def _():
+            tile_copy(e).start()
+
+        @pl.when(index // 2 == a)
+        def _():
+            tiles[index % 2, a] = block(e)[...]
+
+    for k, d in hops(1):
+        hop(d, 1, k).start()
+    deliver(0)
+    for r in range(1, groups):
+        grad_copy(r).start()
+    grads[a] = grad_ref[...]
+    for s in range(1, middle + 1):
+        for k, d in hops(s):
+            hop(d, s, k).wait_recv()
+            if s < middle and (k, d) in hops(s + 1):
+                hop(d, s + 1, k).start()
+        for e in [2 * s - 1, 2 * s] if s < middle else [n - 1]:
+            deliver(e)
+
+    for r in range(1, groups):
+        grad_copy(r).wait_recv()
+        for k in range(2):
+            pltpu.make_async_remote_copy(
+                src_ref=act_ref, dst_ref=tiles.at[k, peers[r]],
+                send_sem=t_send.at[0], recv_sem=t_recv.at[k, peers[r]],
+                device_id={"aa": peers[r]}, device_id_type=MESH,
+            ).wait_recv()
+    act_out[...] = tiles[...]
+    grad_out[...] = grads[...]
+    for s in range(1, middle + 1):
+        for k, d in hops(s):
+            hop(d, s, k).wait_send()
+    for r in range(1, groups):
+        grad_copy(r).wait_send()
+    for e in range(n):
+        @pl.when(owner(e) // 2 != a)
+        def _():
+            tile_copy(e).wait_send()
+
+
+def kernel_gradient(activations, out_grad, n, groups):
+    tokens, features = activations.shape
+    width = out_grad.shape[1]
+    middle = n // 2
+    dma = pltpu.SemaphoreType.DMA
+    vmem = pl.BlockSpec(memory_space=pltpu.VMEM)
+    tiles, grads = pl.pallas_call(
+        functools.partial(tokens_kernel, n, groups),
+        out_shape=(
+            jax.ShapeDtypeStruct((2, groups, tokens, features), jnp.bfloat16),
+            jax.ShapeDtypeStruct((groups, tokens, width), jnp.bfloat16),
+        ),
+        in_specs=[vmem, vmem],
+        out_specs=(vmem, vmem),
+        scratch_shapes=[
+            pltpu.VMEM((n, tokens, features), jnp.bfloat16),
+            pltpu.VMEM((2, groups, tokens, features), jnp.bfloat16),
+            pltpu.VMEM((groups, tokens, width), jnp.bfloat16),
+            dma((2, middle, 2)), dma((2, middle, 2)),
+            dma((n,)), dma((2, groups)), dma((groups,)), dma((groups,)),
+        ],
+        compiler_params=pltpu.CompilerParams(
+            collective_id=1, has_side_effects=True, vmem_limit_bytes=48 * 1024 * 1024
+        ),
+        name="tokens",
+    )(activations, out_grad)
+    grads = grads.reshape(groups * tokens, width)
+    tiles = tiles.reshape(2, groups * tokens, features)
+    return jnp.concatenate([inner_rows(tiles[k], grads) for k in range(2)], axis=0)
+
+
+def plain_gradient(activations, out_grad):
+    features = lax.all_to_all(
+        lax.all_gather(activations, "ba", axis=1, tiled=True),
+        "aa", split_axis=1, concat_axis=0, tiled=True,
+    )
+    return inner_rows(features, lax.all_gather(out_grad, "aa", axis=0, tiled=True))
+
+
 def plain_direction(scaled):
     row_panel = lax.all_gather(scaled, "ba", axis=1, tiled=True)
     gram_part = inner_rows(row_panel, scaled)
@@ -255,21 +401,20 @@
 
 
 def per_device(activations, out_grad, momentum, weight, norm_scale, step_size):
-    features = lax.all_to_all(
-        lax.all_gather(activations, "ba", axis=1, tiled=True),
-        "aa", split_axis=1, concat_axis=0, tiled=True,
-    )
-    gradient = inner_rows(features, lax.all_gather(out_grad, "aa", axis=0, tiled=True))
-    new_momentum = 0.95 * momentum + gradient
-    scaled = (new_momentum / norm_scale).astype(jnp.bfloat16)
     n, groups = lax.axis_size("ba"), lax.axis_size("aa")
-    rows, width = scaled.shape
+    rows, width = momentum.shape
     fits = (
         n % 2 == 0 and n >= 4 and width % 128 == 0
         and width % (16 * groups) == 0 and rows % 32 == 0 and groups == 4
         and (width // groups) % 128 == 0
         and 4 * n * rows * width + 9 * n * width * width + 9 * rows * width < 56 * 2**20
     )
+    if fits and n == 2 * groups and activations.shape[0] % 32 == 0:
+        gradient = kernel_gradient(activations, out_grad, n, groups)
+    else:
+        gradient = plain_gradient(activations, out_grad)
+    new_momentum = 0.95 * momentum + gradient
+    scaled = (new_momentum / norm_scale).astype(jnp.bfloat16)
     direction = fused_direction(scaled, n, groups) if fits else plain_direction(scaled)
     factor = 0.2 * math.sqrt(max(ROWS, COLS))
     new_weight = weight - step_size * factor * direction

time: 320 us -> 266 us (0.83)
  waiting for transfers between devices: 86.1 us -> 0 us
  Pallas kernels: 202 us -> 252 us
  between operations: 16.8 us -> 1.98 us
  starting transfers between devices: 3.69 us -> 0 us
  other arithmetic: 4.11 us -> 7.63 us
    all_gather x2 -> x0, waiting for transfers between devices: 54.8 us -> none  [the longest x1 54.8 us: per_device(): lax.all_gather(activations, 'ba', axis=1, tiled=True)]
    pallas_call x0 -> x1, Pallas kernels: none -> 48 us  [kernel_gradient(): pl.pallas_call(functools.partial(tokens_kernel, n, groups), out_shape=(ja...]
    all_to_all x1 -> x0, waiting for transfers between devices: 30.1 us -> none  [per_device(): lax.all_to_all(lax.all_gather(activations, 'ba', axis=1, tiled=True), 'aa...]
    all_to_all x1 -> x0, starting transfers between devices: 3.61 us -> none  [per_device(): lax.all_to_all(lax.all_gather(activations, 'ba', axis=1, tiled=True), 'aa...]
    convert_element_type x0 -> x1, other arithmetic: none -> 3.52 us  [per_device(): scaled = (new_momentum / norm_scale).astype(jnp.bfloat16)]
  transfers between devices with their start and end apart: 3 -> 0, of which waited for: 2 -> 0; matrix products, arithmetic and copies ran while one was open for 1% -> 0% of each run, Pallas kernels for 0% -> 0%
where the time goes in v2:
time: 266 us
  Pallas kernels  252 us (95%)
  other arithmetic  7.63 us (3%)
    pallas_call x1, Pallas kernels, fused_direction(): pl.pallas_call(functools.partial(powers_kernel, n, groups), out_shape=jax...  203 us
    pallas_call x1, Pallas kernels, kernel_gradient(): pl.pallas_call(functools.partial(tokens_kernel, n, groups), out_shape=(ja...  48 us

profile of v2, /device:TPU:0, one launch (start us, length us, event | category | flops | bytes accessed | tf_op | source)
XLA Modules:
  0.0 266.0 jit_solution(10235190160216804762)
XLA Ops:
  0.6 1.2 copy.8.act_ref
  1.8 0.0 copy-start
  1.8 0.9 copy-done
  2.7 48.0 %tokens.1 = (bf16[2,4,256,528]{3,2,1,0:T(8,128)(2,1)S(1)}, bf16[4,256,512]{2,1,0:T(8,128)(2,1)S(1)}) custom-call(bf16[256,528]{1,0:T(8,128)(2,1)S(1)} %copy.8.act_ref, bf16[256,512]{1,0:T(8,128)(2,1)S(1)} %copy-done), custom_call_target="tpu_custom_call" | custom-call | tf_op jit(solution)/shard_map/tokens/pallas_call | solution.py:346
  50.8 0.3 fusion
  51.1 0.8 fusion.1
  51.8 0.0 copy-start.1
  51.9 1.7 fusion.2
  54.2 0.0 copy-done.1
  54.3 3.5 %divide_convert_fusion = (bf16[1056,512]{1,0:T(8,128)(2,1)}, f32[1056,512]{1,0:T(8,128)}) fusion(f32[]{:T(128)S(6)} %copy.9, f32[528,512]{1,0:T(8,128)} %fusion.2, f32[528,512]{1,0:T(8,128)S(1)} %fusion.1, f32[1056,512]{1,0:T(8,128)S(1)} %copy-done.1), kind=kLoop, calls=%fused_computation.2 | loop fusion | flops 2703360 | bytes 7569412 | tf_op jit(solution)/shard_map/convert_element_type | solution.py:417
  57.8 203.5 %powers.1 = f32[1056,512]{1,0:T(8,128)} custom-call(bf16[1056,512]{1,0:T(8,128)(2,1)} %get-tuple-element.6.x_ref), custom_call_target="tpu_custom_call" | custom-call | tf_op jit(solution)/shard_map/powers/pallas_call | solution.py:208
  261.9 4.1 %multiply_subtract_fusion = f32[1056,512]{1,0:T(8,128)} fusion(f32[1056,512]{1,0:T(8,128)} %param.9, f32[1056,512]{1,0:T(8,128)} %powers.1, f32[]{:T(128)S(6)} %mul.15), kind=kLoop, calls=%fused_computation.1 | loop fusion | flops 1081344 | bytes 6488068 | tf_op jit(solution)/shard_map/sub | solution.py:420
Async XLA Ops:
  1.8 1.0 copy-start
  51.8 2.4 copy-start.1
